TPU v7x, 128 devices: a whole 4x4x4 slice. The times are simulated.
128 devices in a mesh: dp: 1, hp: 16 (over z, y), cp: 8 (over x, core).
Axes of the slice: x: 4, y: 4, z: 4, core: 2. Of those that a mesh axis runs over, the one named last changes fastest.
Arguments:
- latent: bfloat16 [96, 16, 48, 512], P(('dp', 'cp'), 'hp')
- conv_w: bfloat16 [4, 3, 3, 3, 512, 512], replicated
- conv_b: float32 [4, 512], replicated
- gn_gamma: float32 [4, 512], replicated
- gn_beta: float32 [4, 512], replicated
Outputs:
- output: bfloat16 [96, 16, 48, 512], P(('dp', 'cp'), 'hp')
All inputs are finite; a program needn't handle non-finite values.
Results may differ from a plain program's by a relative error of at most 0.00972573.
Values are sent between devices in bfloat16 or wider.
A program may use at most 1 GiB of HBM per device.

v0:
```python
import jax
import jax.numpy as jnp
from jax import lax
from jax.sharding import PartitionSpec as P

GROUPS = 32
EPS = 1e-6


def norm_silu(local_act, gamma, beta, total_count):
    frames, row_count, lat_width, channels = local_act.shape
    per_group = channels // GROUPS
    grouped = local_act.reshape(frames, row_count, lat_width, GROUPS, per_group).astype(jnp.float32)
    stat_sums = jnp.stack([jnp.sum(grouped, axis=(0, 1, 2, 4)), jnp.sum(grouped * grouped, axis=(0, 1, 2, 4))])
    stat_sums = lax.psum(stat_sums, ("cp", "hp"))
    mean_val = stat_sums[0] / total_count
    variance = stat_sums[1] / total_count - mean_val * mean_val
    inv_std = lax.rsqrt(variance + EPS)
    gamma_g = gamma.reshape(GROUPS, per_group)
    scale_c = (inv_std[:, None] * gamma_g).reshape(channels)
    shift_c = (beta.reshape(GROUPS, per_group) - (mean_val * inv_std)[:, None] * gamma_g).reshape(channels)
    return jax.nn.silu(local_act.astype(jnp.float32) * scale_c + shift_c).astype(jnp.bfloat16)


def conv_valid(padded, kernel, bias_vec):
    conv_out = lax.conv_general_dilated(padded[None], kernel, (1, 1, 1), ((0, 0), (0, 0), (1, 1)), dimension_numbers=("NDHWC", "DHWIO", "NDHWC"), preferred_element_type=jnp.float32)
    return (conv_out[0] + bias_vec).astype(jnp.bfloat16)


def solution(mesh):
    n_time = mesh.shape["cp"]
    n_rows = mesh.shape["hp"]
    time_fwd = [(i, i + 1) for i in range(n_time - 1)]
    rows_down = [(i, i + 1) for i in range(n_rows - 1)]
    rows_up = [(i + 1, i) for i in range(n_rows - 1)]

    def local_decode(local_lat, conv_w, conv_b, gn_gamma, gn_beta):
        frames, row_count, lat_width, channels = local_lat.shape
        total_count = frames * n_time * row_count * n_rows * lat_width * (channels // GROUPS)
        time_rank = lax.axis_index("cp")
        residual = local_lat
        for block_idx in range(2):
            hidden = residual
            for sub_idx in range(2):
                layer_idx = 2 * block_idx + sub_idx
                activated = norm_silu(hidden, gn_gamma[layer_idx], gn_beta[layer_idx], total_count)
                prev_frames = lax.ppermute(activated[frames - 2:], "cp", time_fwd)
                own_first = jnp.broadcast_to(activated[:1], prev_frames.shape)
                prev_frames = jnp.where(time_rank == 0, own_first, prev_frames)
                extended = jnp.concatenate([prev_frames, activated], axis=0)
                from_above = lax.ppermute(extended[:, row_count - 1:], "hp", rows_down)
                from_below = lax.ppermute(extended[:, :1], "hp", rows_up)
                extended = jnp.concatenate([from_above, extended, from_below], axis=1)
                hidden = conv_valid(extended, conv_w[layer_idx], conv_b[layer_idx])
            residual = (residual.astype(jnp.float32) + hidden.astype(jnp.float32)).astype(jnp.bfloat16)
        return residual

    video_spec = P(("dp", "cp"), "hp", None, None)
    return jax.shard_map(local_decode, mesh=mesh, in_specs=(video_spec, P(), P(), P(), P()), out_specs=video_spec, check_vma=False)
```

profile of v0, /device:TPU:34, one launch (start us, length us, event | category | flops | bytes accessed | tf_op | source)
XLA Modules:
  0.0 556.9 jit_solution(15278008590620678836)
XLA Ops:
  5.1 65.3 %psum.28 = f32[2,32]{1,0:T(2,128)S(1)} all-reduce(f32[2,32]{1,0:T(2,128)S(1)} %pad_maximum_fusion.4), channel_id=1, replica_groups=mesh['dp'=1,'hp'=16,'cp'=8] {'cp','hp'}, use_global_device_ids=true, to_apply=%region_4.5 | all-reduce | flops 64 | bytes 512 | tf_op jit(solution)/shard_map/psum | solution.py:15
  76.8 4.9 collective-permute-done
  83.7 4.8 collective-permute-start.2
  90.7 26.4 %collective-permute-done.2 = bf16[14,1,48,512]{3,1,2,0:T(2,128)(2,1)S(1)} collective-permute-done((bf16[14,1,48,512]{3,1,2,0:T(2,128)(2,1)S(1)}, bf16[14,1,48,512]{3,1,2,0:T(2,128)(2,1)S(1)}, u32[]{:S(2)}, u32[]{:S(2)}) %collective-permute-start.2) | collective-permute-done | bytes 688160 | tf_op jit(solution)/shard_map/ppermute | solution.py:52
  117.1 6.2 %collective-permute-done.1 = bf16[14,1,48,512]{3,1,2,0:T(2,128)(2,1)S(1)} collective-permute-done((bf16[14,1,48,512]{3,1,2,0:T(2,128)(2,1)S(1)}, bf16[14,1,48,512]{3,1,2,0:T(2,128)(2,1)S(1)}, u32[]{:S(2)}, u32[]{:S(2)}) %collective-permute-start.1) | collective-permute-done | bytes 688160 | tf_op jit(solution)/shard_map/ppermute | solution.py:51
  123.4 4.7 maximum_bitcast_fusion
  131.2 13.4 %fusion.44 = (f32[512]{0:T(512)S(1)}, f32[512]{0:T(512)S(1)}, f32[12,1,8,7,512]{4,2,3,1,0:T(8,128)S(1)}) fusion(pred[8,7]{0,1:T(8,128)(4,1)S(1)} %copy-done.2, f32[512]{0:T(512)S(1)} %bitcast.241, bf16[4,3,3,3,512,512]{5,4,3,2,1,0:T(8,128)(2,1)} %param.6, bf16[14,3,1,7,2,512]{5,3,4,1,0,2:T(8,128)(2,1)S(1)} %slice.138, ...), kind=kOutput, calls=%fused_computation.49 | convolution fusion | flops 9525067776 | bytes 18548792 | tf_op jit(solution)/shard_map/conv_general_dilated | solution.py:26
  145.0 60.8 %psum.29 = f32[2,32]{1,0:T(2,128)S(1)} all-reduce(f32[2,32]{1,0:T(2,128)S(1)} %pad_maximum_fusion.5), channel_id=1, replica_groups=mesh['dp'=1,'hp'=16,'cp'=8] {'cp','hp'}, use_global_device_ids=true, to_apply=%region_9.10 | all-reduce | flops 64 | bytes 512 | tf_op jit(solution)/shard_map/psum | solution.py:15
  212.7 4.9 collective-permute-done.3
  226.7 26.3 %collective-permute-done.5 = bf16[14,1,48,512]{3,1,2,0:T(2,128)(2,1)S(1)} collective-permute-done((bf16[14,1,48,512]{3,1,2,0:T(2,128)(2,1)S(1)}, bf16[14,1,48,512]{3,1,2,0:T(2,128)(2,1)S(1)}, u32[]{:S(2)}, u32[]{:S(2)}) %collective-permute-start.5) | collective-permute-done | bytes 688160 | tf_op jit(solution)/shard_map/ppermute | solution.py:52
  252.9 6.2 %collective-permute-done.4 = bf16[14,1,48,512]{3,1,2,0:T(2,128)(2,1)S(1)} collective-permute-done((bf16[14,1,48,512]{3,1,2,0:T(2,128)(2,1)S(1)}, bf16[14,1,48,512]{3,1,2,0:T(2,128)(2,1)S(1)}, u32[]{:S(2)}, u32[]{:S(2)}) %collective-permute-start.4) | collective-permute-done | bytes 688160 | tf_op jit(solution)/shard_map/ppermute | solution.py:51
  259.2 4.7 maximum_bitcast_fusion.1
  266.5 13.1 %fusion.55 = f32[12,1,8,7,512]{4,2,3,1,0:T(8,128)S(1)} fusion(bf16[4,3,3,3,512,512]{5,4,3,2,1,0:T(8,128)(2,1)} %param.6, bf16[14,3,1,7,2,512]{5,3,4,1,0,2:T(8,128)(2,1)S(1)} %slice.142, bf16[14,3,1,8,7,512]{5,3,4,1,0,2:T(8,128)(2,1)S(1)} %copy.13, pred[8,7]{0,1:T(8,128)(4,1)S(1)} %copy-done.2), kind=kOutput, calls=%fused_computation.62 | convolution fusion | flops 9522315264 | bytes 18542648 | tf_op jit(solution)/shard_map/conv_general_dilated | solution.py:26
  284.2 60.7 %psum.30 = f32[2,32]{1,0:T(2,128)S(1)} all-reduce(f32[2,32]{1,0:T(2,128)S(1)} %pad_maximum_fusion.6), channel_id=1, replica_groups=mesh['dp'=1,'hp'=16,'cp'=8] {'cp','hp'}, use_global_device_ids=true, to_apply=%region_14.15 | all-reduce | flops 64 | bytes 512 | tf_op jit(solution)/shard_map/psum | solution.py:15
  350.4 4.9 collective-permute-done.6
  363.9 26.4 %collective-permute-done.8 = bf16[14,1,48,512]{3,1,2,0:T(2,128)(2,1)S(1)} collective-permute-done((bf16[14,1,48,512]{3,1,2,0:T(2,128)(2,1)S(1)}, bf16[14,1,48,512]{3,1,2,0:T(2,128)(2,1)S(1)}, u32[]{:S(2)}, u32[]{:S(2)}) %collective-permute-start.8) | collective-permute-done | bytes 688160 | tf_op jit(solution)/shard_map/ppermute | solution.py:52
  390.3 6.2 %collective-permute-done.7 = bf16[14,1,48,512]{3,1,2,0:T(2,128)(2,1)S(1)} collective-permute-done((bf16[14,1,48,512]{3,1,2,0:T(2,128)(2,1)S(1)}, bf16[14,1,48,512]{3,1,2,0:T(2,128)(2,1)S(1)}, u32[]{:S(2)}, u32[]{:S(2)}) %collective-permute-start.7) | collective-permute-done | bytes 688160 | tf_op jit(solution)/shard_map/ppermute | solution.py:51
  403.9 13.4 %fusion.47 = (f32[512]{0:T(512)S(1)}, f32[512]{0:T(512)S(1)}, f32[12,1,8,7,512]{4,2,3,1,0:T(8,128)S(1)}) fusion(pred[8,7]{0,1:T(8,128)(4,1)S(1)} %copy-done.2, f32[512]{0:T(512)S(1)} %bitcast.239, bf16[4,3,3,3,512,512]{5,4,3,2,1,0:T(8,128)(2,1)} %param.6, bf16[14,3,1,7,2,512]{5,3,4,1,0,2:T(8,128)(2,1)S(1)} %slice.146, ...), kind=kOutput, calls=%fused_computation.52 | convolution fusion | flops 9525067776 | bytes 18548792 | tf_op jit(solution)/shard_map/conv_general_dilated | solution.py:26
  417.7 60.8 %psum.31 = f32[2,32]{1,0:T(2,128)S(1)} all-reduce(f32[2,32]{1,0:T(2,128)S(1)} %pad_maximum_fusion.7), channel_id=1, replica_groups=mesh['dp'=1,'hp'=16,'cp'=8] {'cp','hp'}, use_global_device_ids=true, to_apply=%region_19.20 | all-reduce | flops 64 | bytes 512 | tf_op jit(solution)/shard_map/psum | solution.py:15
  485.3 5.0 collective-permute-done.9
  499.1 26.6 %collective-permute-done.11 = bf16[14,1,48,512]{3,1,2,0:T(2,128)(2,1)S(1)} collective-permute-done((bf16[14,1,48,512]{3,1,2,0:T(2,128)(2,1)S(1)}, bf16[14,1,48,512]{3,1,2,0:T(2,128)(2,1)S(1)}, u32[]{:S(2)}, u32[]{:S(2)}) %collective-permute-start.11) | collective-permute-done | bytes 688160 | tf_op jit(solution)/shard_map/ppermute | solution.py:52
  525.7 6.2 %collective-permute-done.10 = bf16[14,1,48,512]{3,1,2,0:T(2,128)(2,1)S(1)} collective-permute-done((bf16[14,1,48,512]{3,1,2,0:T(2,128)(2,1)S(1)}, bf16[14,1,48,512]{3,1,2,0:T(2,128)(2,1)S(1)}, u32[]{:S(2)}, u32[]{:S(2)}) %collective-permute-start.10) | collective-permute-done | bytes 688160 | tf_op jit(solution)/shard_map/ppermute | solution.py:51
  531.9 4.7 maximum_bitcast_fusion.3
  539.3 13.1 %fusion.65 = f32[12,1,8,7,512]{4,2,3,1,0:T(8,128)S(1)} fusion(bf16[4,3,3,3,512,512]{5,4,3,2,1,0:T(8,128)(2,1)} %param.6, bf16[14,3,1,7,2,512]{5,3,4,1,0,2:T(8,128)(2,1)S(1)} %slice.150, bf16[14,3,1,8,7,512]{5,3,4,1,0,2:T(8,128)(2,1)S(1)} %copy.23, pred[8,7]{0,1:T(8,128)(4,1)S(1)} %copy-done.2), kind=kOutput, calls=%fused_computation.64 | convolution fusion | flops 9522315264 | bytes 18542648 | tf_op jit(solution)/shard_map/conv_general_dilated | solution.py:26
  (109 shorter events, 85.8 us)
Async XLA Ops:
  74.7 7.0 %collective-permute-start = (bf16[2,1,48,512]{3,1,2,0:T(2,128)(2,1)S(1)}, bf16[2,1,48,512]{3,1,2,0:T(2,128)(2,1)S(1)}, u32[]{:S(2)}, u32[]{:S(2)}) collective-permute-start(bf16[2,1,48,512]{3,1,2,0:T(2,128)(2,1)S(1)} %slice.137), channel_id=1, source_target_pairs={{0,1},{1,2},{2,3},{3,4},{4,5},{5,6},{6,7},{8,9},{9,10},{10,11},{11... | collective-permute-start | bytes 294920 | tf_op jit(solution)/shard_map/ppermute | solution.py:47
  81.9 8.8 %copy-start.1 = (f32[4,512]{1,0:T(4,128)S(1)}, f32[4,512]{1,0:T(4,128)}, u32[]{:S(2)}) copy-start(f32[4,512]{1,0:T(4,128)} %param.7) | copy-start | bytes 24580
  83.7 33.4 %collective-permute-start.2 = (bf16[14,1,48,512]{3,1,2,0:T(2,128)(2,1)S(1)}, bf16[14,1,48,512]{3,1,2,0:T(2,128)(2,1)S(1)}, u32[]{:S(2)}, u32[]{:S(2)}) collective-permute-start(bf16[14,1,48,512]{3,1,2,0:T(2,128)(2,1)S(1)} %pad_maximum_fusion), channel_id=1, source_target_pairs={{8,0},{16,8},{24,16},{32,24},{40,32},{48,40},{56,48},{64,56},{72,6... | collective-permute-start | bytes 2064392 | tf_op jit(solution)/shard_map/ppermute | solution.py:52
  88.6 34.8 %collective-permute-start.1 = (bf16[14,1,48,512]{3,1,2,0:T(2,128)(2,1)S(1)}, bf16[14,1,48,512]{3,1,2,0:T(2,128)(2,1)S(1)}, u32[]{:S(2)}, u32[]{:S(2)}) collective-permute-start(bf16[14,1,48,512]{3,1,2,0:T(2,128)(2,1)S(1)} %pad_maximum_fusion), channel_id=1, source_target_pairs={{0,8},{8,16},{16,24},{24,32},{32,40},{40,48},{48,56},{56,64},{64,7... | collective-permute-start | bytes 2064392 | tf_op jit(solution)/shard_map/ppermute | solution.py:51
  130.5 0.7 copy-start.2
  210.6 7.0 %collective-permute-start.3 = (bf16[2,1,48,512]{3,1,2,0:T(2,128)(2,1)S(1)}, bf16[2,1,48,512]{3,1,2,0:T(2,128)(2,1)S(1)}, u32[]{:S(2)}, u32[]{:S(2)}) collective-permute-start(bf16[2,1,48,512]{3,1,2,0:T(2,128)(2,1)S(1)} %slice.141), channel_id=1, source_target_pairs={{0,1},{1,2},{2,3},{3,4},{4,5},{5,6},{6,7},{8,9},{9,10},{10,11},{11... | collective-permute-start | bytes 294920 | tf_op jit(solution)/shard_map/ppermute | solution.py:47
  219.7 33.3 %collective-permute-start.5 = (bf16[14,1,48,512]{3,1,2,0:T(2,128)(2,1)S(1)}, bf16[14,1,48,512]{3,1,2,0:T(2,128)(2,1)S(1)}, u32[]{:S(2)}, u32[]{:S(2)}) collective-permute-start(bf16[14,1,48,512]{3,1,2,0:T(2,128)(2,1)S(1)} %pad_maximum_fusion.1), channel_id=1, source_target_pairs={{8,0},{16,8},{24,16},{32,24},{40,32},{48,40},{56,48},{64,56},{72,6... | collective-permute-start | bytes 2064392 | tf_op jit(solution)/shard_map/ppermute | solution.py:52
  224.3 34.9 %collective-permute-start.4 = (bf16[14,1,48,512]{3,1,2,0:T(2,128)(2,1)S(1)}, bf16[14,1,48,512]{3,1,2,0:T(2,128)(2,1)S(1)}, u32[]{:S(2)}, u32[]{:S(2)}) collective-permute-start(bf16[14,1,48,512]{3,1,2,0:T(2,128)(2,1)S(1)} %pad_maximum_fusion.1), channel_id=1, source_target_pairs={{0,8},{8,16},{16,24},{24,32},{32,40},{40,48},{48,56},{56,64},{64,7... | collective-permute-start | bytes 2064392 | tf_op jit(solution)/shard_map/ppermute | solution.py:51
  279.7 1.4 copy-start
  348.3 7.0 %collective-permute-start.6 = (bf16[2,1,48,512]{3,1,2,0:T(2,128)(2,1)S(1)}, bf16[2,1,48,512]{3,1,2,0:T(2,128)(2,1)S(1)}, u32[]{:S(2)}, u32[]{:S(2)}) collective-permute-start(bf16[2,1,48,512]{3,1,2,0:T(2,128)(2,1)S(1)} %slice.145), channel_id=1, source_target_pairs={{0,1},{1,2},{2,3},{3,4},{4,5},{5,6},{6,7},{8,9},{9,10},{10,11},{11... | collective-permute-start | bytes 294920 | tf_op jit(solution)/shard_map/ppermute | solution.py:47
  357.3 33.0 %collective-permute-start.8 = (bf16[14,1,48,512]{3,1,2,0:T(2,128)(2,1)S(1)}, bf16[14,1,48,512]{3,1,2,0:T(2,128)(2,1)S(1)}, u32[]{:S(2)}, u32[]{:S(2)}) collective-permute-start(bf16[14,1,48,512]{3,1,2,0:T(2,128)(2,1)S(1)} %pad_maximum_fusion.2), channel_id=1, source_target_pairs={{8,0},{16,8},{24,16},{32,24},{40,32},{48,40},{56,48},{64,56},{72,6... | collective-permute-start | bytes 2064392 | tf_op jit(solution)/shard_map/ppermute | solution.py:52
  361.9 34.6 %collective-permute-start.7 = (bf16[14,1,48,512]{3,1,2,0:T(2,128)(2,1)S(1)}, bf16[14,1,48,512]{3,1,2,0:T(2,128)(2,1)S(1)}, u32[]{:S(2)}, u32[]{:S(2)}) collective-permute-start(bf16[14,1,48,512]{3,1,2,0:T(2,128)(2,1)S(1)} %pad_maximum_fusion.2), channel_id=1, source_target_pairs={{0,8},{8,16},{16,24},{24,32},{32,40},{40,48},{48,56},{56,64},{64,7... | collective-permute-start | bytes 2064392 | tf_op jit(solution)/shard_map/ppermute | solution.py:51
  483.3 7.1 %collective-permute-start.9 = (bf16[2,1,48,512]{3,1,2,0:T(2,128)(2,1)S(1)}, bf16[2,1,48,512]{3,1,2,0:T(2,128)(2,1)S(1)}, u32[]{:S(2)}, u32[]{:S(2)}) collective-permute-start(bf16[2,1,48,512]{3,1,2,0:T(2,128)(2,1)S(1)} %slice.149), channel_id=1, source_target_pairs={{0,1},{1,2},{2,3},{3,4},{4,5},{5,6},{6,7},{8,9},{9,10},{10,11},{11... | collective-permute-start | bytes 294920 | tf_op jit(solution)/shard_map/ppermute | solution.py:47
  492.4 33.3 %collective-permute-start.11 = (bf16[14,1,48,512]{3,1,2,0:T(2,128)(2,1)S(1)}, bf16[14,1,48,512]{3,1,2,0:T(2,128)(2,1)S(1)}, u32[]{:S(2)}, u32[]{:S(2)}) collective-permute-start(bf16[14,1,48,512]{3,1,2,0:T(2,128)(2,1)S(1)} %pad_maximum_fusion.3), channel_id=1, source_target_pairs={{8,0},{16,8},{24,16},{32,24},{40,32},{48,40},{56,48},{64,56},{72,6... | collective-permute-start | bytes 2064392 | tf_op jit(solution)/shard_map/ppermute | solution.py:52
  496.9 35.0 %collective-permute-start.10 = (bf16[14,1,48,512]{3,1,2,0:T(2,128)(2,1)S(1)}, bf16[14,1,48,512]{3,1,2,0:T(2,128)(2,1)S(1)}, u32[]{:S(2)}, u32[]{:S(2)}) collective-permute-start(bf16[14,1,48,512]{3,1,2,0:T(2,128)(2,1)S(1)} %pad_maximum_fusion.3), channel_id=1, source_target_pairs={{0,8},{8,16},{16,24},{24,32},{32,40},{40,48},{48,56},{56,64},{64,7... | collective-permute-start | bytes 2064392 | tf_op jit(solution)/shard_map/ppermute | solution.py:51
where the time goes:
time: 564 us; the launch traced here: 557 us
  blocking collectives  248 us (44%)
  waiting for transfers between devices  150 us (27%)
  matrix products  53 us (9%)
  other arithmetic  47.4 us (8%)
  starting transfers between devices  34.9 us (6%)
  local copies, waits for them, and re-layouts  22.4 us (4%)
    psum x4, blocking collectives, norm_silu(): stat_sums = lax.psum(stat_sums, ('cp', 'hp'))  248 us
    ppermute x4, waiting for transfers between devices, local_decode(): from_below = lax.ppermute(extended[:, :1], 'hp', rows_up)  106 us
    conv_general_dilated x4, matrix products, conv_valid(): lax.conv_general_dilated(padded[None], kernel, (1, 1, 1), ((0, 0), (0, 0)...  53 us
    ppermute x4, waiting for transfers between devices, local_decode(): from_above = lax.ppermute(extended[:, row_count - 1:], 'hp', rows_down)  25 us
    ppermute x4, waiting for transfers between devices, local_decode(): prev_frames = lax.ppermute(activated[frames - 2:], 'cp', time_fwd)  19.8 us
    broadcast_in_dim x4, other arithmetic, conv_valid(): padded[None]  18.8 us
    ppermute x4, starting transfers between devices, local_decode(): from_below = lax.ppermute(extended[:, :1], 'hp', rows_up)  18.6 us
    convert_element_type x4, other arithmetic, norm_silu(): jax.nn.silu(local_act.astype(jnp.float32) * scale_c + shift_c)  12.2 us
  transfers between devices with their start and end apart: 12, of which 12 were waited for; matrix products, arithmetic and copies ran while one was open for 0% of the time, Pallas kernels for 0%

commit v1 on v0

v1 whole, which is shorter than its diff:
```python
import functools

import jax
import jax.numpy as jnp
from jax import lax
from jax.experimental import pallas as pl
from jax.experimental.pallas import tpu as pltpu
from jax.sharding import PartitionSpec as P

GROUPS = 32
EPS = 1e-6
LAYERS = 4
MESH = pl.DeviceIdType.MESH
CHUNK = 3


def lane_sums(y, lane):
    for d in (8, 4, 2, 1):
        y = y + jnp.where((lane & d) != 0, pltpu.roll(y, d, 1), pltpu.roll(y, 128 - d, 1))
    return y


def decode_kernel(n_hp, n_cp, total_count, lat_ref, w_ref, b_ref, g_ref, be_ref, o_ref,
                  wbuf, raw, act, acc, xres, ssum, st8, coef, msg_a, msg_b, st_a, st_b,
                  w_sem, lat_sem, send_sem, recv_sem, ssend_a, srecv_a, ssend_b, srecv_b):
    frames, width, channels = xres.shape
    n_chunks = frames // CHUNK
    hp = lax.axis_index("hp")
    cp = lax.axis_index("cp")
    has_up = hp > 0
    has_down = hp < n_hp - 1
    has_next = cp < n_cp - 1
    has_prev = cp > 0

    slab_order = [(k, 1) for k in range(3)] + [(k, di) for di in (0, 2) for k in range(3)]

    def weight_copy(layer, slot, k, di):
        slab = k * 3 + di
        return pltpu.make_async_copy(w_ref.at[layer, slab], wbuf.at[slot, slab], w_sem.at[slot, slab])

    def start_weights(layer, slot):
        for k, di in slab_order:
            weight_copy(layer, slot, k, di).start()

    lat_copies = [pltpu.make_async_copy(lat_ref, raw.at[0, 1, pl.ds(2, frames)], lat_sem.at[0]),
                  pltpu.make_async_copy(lat_ref, xres, lat_sem.at[1])]
    for copy in lat_copies:
        copy.start()
    start_weights(0, 0)

    barrier = pltpu.get_barrier_semaphore()

    @pl.loop(1, n_cp)
    def _(i):
        pl.semaphore_signal(barrier, inc=1, device_id={"cp": lax.rem(cp + i, n_cp)}, device_id_type=MESH)

    @pl.loop(1, n_hp)
    def _(i):
        pl.semaphore_signal(barrier, inc=1, device_id={"hp": lax.rem(hp + i, n_hp)}, device_id_type=MESH)

    for dh, ok_h in ((-1, has_up), (1, has_down)):
        for dc, ok_c in ((-1, has_prev), (1, has_next)):
            @pl.when(jnp.logical_and(ok_h, ok_c))
            def _():
                pl.semaphore_signal(barrier, inc=1, device_id={"hp": hp + dh, "cp": cp + dc}, device_id_type=MESH)

    n_rows = has_up.astype(jnp.int32) + has_down.astype(jnp.int32)
    n_times = has_prev.astype(jnp.int32) + has_next.astype(jnp.int32)
    pl.semaphore_wait(barrier, n_cp - 1 + n_hp - 1 + n_rows * n_times)

    def row_copy(slot, c, to_down):
        span = pl.ds(2 + c * CHUNK, CHUNK)
        row = 0 if to_down else 2
        return pltpu.make_async_remote_copy(
            src_ref=raw.at[slot, 1, span], dst_ref=raw.at[slot, row, span],
            send_sem=send_sem.at[row, c], recv_sem=recv_sem.at[slot, row, c],
            device_id={"hp": hp + (1 if to_down else -1)}, device_id_type=MESH)

    def time_copy(slot, dh):
        row = dh if dh is None else (0 if dh == 1 else 2)
        row = 1 if dh == 0 else row
        return pltpu.make_async_remote_copy(
            src_ref=raw.at[slot, 1, pl.ds(frames, 2)], dst_ref=raw.at[slot, row, pl.ds(0, 2)],
            send_sem=send_sem.at[row, n_chunks], recv_sem=recv_sem.at[slot, row, n_chunks],
            device_id={"hp": hp + dh, "cp": cp + 1}, device_id_type=MESH)

    def start_rows(slot, c):
        @pl.when(has_up)
        def _():
            row_copy(slot, c, False).start()

        @pl.when(has_down)
        def _():
            row_copy(slot, c, True).start()

    def start_times(slot):
        @pl.when(has_next)
        def _():
            time_copy(slot, 0).start()

        @pl.when(jnp.logical_and(has_next, has_up))
        def _():
            time_copy(slot, -1).start()

        @pl.when(jnp.logical_and(has_next, has_down))
        def _():
            time_copy(slot, 1).start()

    def wait_sends(slot):
        for c in range(n_chunks):
            @pl.when(has_up)
            def _():
                row_copy(slot, c, False).wait_send()

            @pl.when(has_down)
            def _():
                row_copy(slot, c, True).wait_send()

        @pl.when(has_next)
        def _():
            time_copy(slot, 0).wait_send()

        @pl.when(jnp.logical_and(has_next, has_up))
        def _():
            time_copy(slot, -1).wait_send()

        @pl.when(jnp.logical_and(has_next, has_down))
        def _():
            time_copy(slot, 1).wait_send()

    for copy in lat_copies:
        copy.wait()
    start_times(0)
    for c in range(n_chunks):
        start_rows(0, c)

    for row, ok in ((0, has_up), (2, has_down)):
        @pl.when(jnp.logical_not(ok))
        def _():
            @pl.loop(0, frames + 2)
            def _(f):
                act[row, f] = jnp.zeros((width, 3 * channels), jnp.bfloat16)

    def fold(v):
        return jnp.sum(v.reshape(-1, 8, v.shape[-1]), axis=0)

    ssum[...] = jnp.zeros_like(ssum)

    @pl.loop(0, frames)
    def _(f):
        v = xres[f].astype(jnp.float32)
        ssum[0] += fold(v)
        ssum[1] += fold(v * v)

    lane = lax.broadcasted_iota(jnp.int32, (8, 128), 1)
    sub = lax.broadcasted_iota(jnp.int32, (8, 128), 0)
    pick = (lane & 15) == sub

    def exchange(layer, axis, n, me, msg, st, send, recv):
        @pl.loop(1, n)
        def _(i):
            pltpu.make_async_remote_copy(
                src_ref=msg.at[layer], dst_ref=st.at[layer, me], send_sem=send.at[layer], recv_sem=recv.at[layer],
                device_id={axis: lax.rem(me + i, n)}, device_id_type=MESH).start()

        st[layer, me] = msg[layer]
        rest = st.at[layer, pl.ds(0, n - 1)]
        pltpu.make_async_copy(rest, rest, recv.at[layer]).wait()
        pltpu.make_async_copy(rest, rest, send.at[layer]).wait()
        return jnp.sum(st[layer], axis=0)

    def statistics(layer):
        for s in range(2):
            for i in range(4):
                st8[s * 4 + i : s * 4 + i + 1, :] = jnp.sum(ssum[s, :, i * 128 : (i + 1) * 128], axis=0, keepdims=True)
        mine = jnp.where(pick, lane_sums(st8[...], lane), 0.0)
        msg_a[layer] = jnp.sum(mine, axis=0, keepdims=True)
        msg_b[layer] = exchange(layer, "cp", n_cp, cp, msg_a, st_a, ssend_a, srecv_a)
        total = exchange(layer, "hp", n_hp, hp, msg_b, st_b, ssend_b, srecv_b)
        st8[...] = lane_sums(jnp.where(pick, jnp.broadcast_to(total, (8, 128)), 0.0), lane)
        mean = st8[0:4, :] / total_count
        var = st8[4:8, :] / total_count - mean * mean
        inv = lax.rsqrt(var + EPS)
        scale = g_ref[layer] * inv
        shift = be_ref[layer] - (mean * inv) * g_ref[layer]
        for i in range(4):
            coef[0:1, i * 128 : (i + 1) * 128] = 0.5 * scale[i : i + 1, :]
            coef[1:2, i * 128 : (i + 1) * 128] = 0.5 * shift[i : i + 1, :]

    first_frame = jnp.where(has_prev, 0, 2)
    col = lax.broadcasted_iota(jnp.int32, (width, channels), 0)

    def activate(slot, row, f):
        v = raw[slot, row, jnp.maximum(f, first_frame)].astype(jnp.float32)
        u = v * coef[0:1, :] + coef[1:2, :]
        y = u * jnp.tanh(u) + u
        left = jnp.where(col == 0, 0.0, pltpu.roll(y, 1, 0))
        right = jnp.where(col == width - 1, 0.0, pltpu.roll(y, width - 1, 0))
        for dj, v in enumerate((left, y, right)):
            act[row, f, :, dj * channels : (dj + 1) * channels] = v.astype(jnp.bfloat16)

    def taps(slot, di, start, count):
        total = None
        for d in di:
            for k in range(3):
                lhs = act[d, pl.ds(start + k, count)].reshape(count * width, 3 * channels)
                part = jnp.dot(lhs, wbuf[slot, k * 3 + d], preferred_element_type=jnp.float32)
                total = part if total is None else total + part
        return total

    def layer_body(layer, _):
        slot = lax.rem(layer, 2)
        other = 1 - slot

        @pl.when(layer < LAYERS - 1)
        def _():
            start_weights(layer + 1, other)

        statistics(layer)

        @pl.when(has_prev)
        def _():
            time_copy(slot, 0).wait_recv()

        @pl.loop(0, frames + 2)
        def _(f):
            activate(slot, 1, f)

        for k, di in slab_order:
            weight_copy(layer, slot, k, di).wait()

        half = frames // 2

        @pl.loop(0, 2)
        def _(h):
            acc[pl.ds(h * half, half)] = taps(slot, (1,), h * half, half).reshape(half, width, channels)

        for row, ok in ((0, has_up), (2, has_down)):
            @pl.when(ok)
            def _():
                @pl.when(has_prev)
                def _():
                    time_copy(slot, 1 if row == 0 else -1).wait_recv()

                for c in range(n_chunks):
                    row_copy(slot, c, row == 0).wait_recv()

                @pl.loop(0, frames + 2)
                def _(f):
                    activate(slot, row, f)

        wait_sends(slot)
        ssum[...] = jnp.zeros_like(ssum)
        second = lax.rem(layer, 2) == 1
        bias = b_ref[layer]
        @pl.loop(0, n_chunks)
        def _(c):
            span = pl.ds(c * CHUNK, CHUNK)
            y = taps(slot, (0, 2), c * CHUNK, CHUNK).reshape(CHUNK, width, channels)
            h = (acc[span] + y + bias).astype(jnp.bfloat16).astype(jnp.float32)
            x = xres[span].astype(jnp.float32)
            out = (h + jnp.where(second, x, 0.0)).astype(jnp.bfloat16)
            raw[other, 1, pl.ds(2 + c * CHUNK, CHUNK)] = out
            out = out.astype(jnp.float32)
            xres[span] = jnp.where(second, out, x).astype(jnp.bfloat16)
            ssum[0] += fold(out)
            ssum[1] += fold(out * out)

            @pl.when(layer < LAYERS - 1)
            def _():
                start_rows(other, c)

        @pl.when(layer < LAYERS - 1)
        def _():
            start_times(other)

        return 0

    lax.fori_loop(0, LAYERS, layer_body, 0)

    @pl.loop(0, frames)
    def _(f):
        o_ref[f] = xres[f]


def solution(mesh):
    n_hp, n_cp = mesh.shape["hp"], mesh.shape["cp"]

    def local_decode(lat, conv_w, conv_b, gn_gamma, gn_beta):
        frames, rows, width, channels = lat.shape
        n_chunks = frames // CHUNK
        total_count = float(frames * n_cp * rows * n_hp * width * (channels // GROUPS))
        any_spec = pl.BlockSpec(memory_space=pl.ANY)
        vmem_spec = pl.BlockSpec(memory_space=pltpu.VMEM)
        bf16, f32 = jnp.bfloat16, jnp.float32
        flops = LAYERS * 2 * frames * width * 27 * channels * channels
        out = pl.pallas_call(
            functools.partial(decode_kernel, n_hp, n_cp, total_count),
            out_shape=jax.ShapeDtypeStruct((frames, width, channels), bf16),
            in_specs=[any_spec, any_spec, vmem_spec, vmem_spec, vmem_spec],
            out_specs=vmem_spec,
            scratch_shapes=[
                pltpu.VMEM((2, 9, 3 * channels, channels), bf16),
                pltpu.VMEM((2, 3, frames + 2, width, channels), bf16),
                pltpu.VMEM((3, frames + 2, width, 3 * channels), bf16),
                pltpu.VMEM((frames, width, channels), f32),
                pltpu.VMEM((frames, width, channels), bf16),
                pltpu.VMEM((2, 8, channels), f32),
                pltpu.VMEM((8, 128), f32),
                pltpu.VMEM((8, channels), f32),
                pltpu.VMEM((LAYERS, 1, 128), f32),
                pltpu.VMEM((LAYERS, 1, 128), f32),
                pltpu.VMEM((LAYERS, n_cp, 1, 128), f32),
                pltpu.VMEM((LAYERS, n_hp, 1, 128), f32),
                pltpu.SemaphoreType.DMA((2, 9)),
                pltpu.SemaphoreType.DMA((2,)),
                pltpu.SemaphoreType.DMA((3, n_chunks + 1)),
                pltpu.SemaphoreType.DMA((2, 3, n_chunks + 1)),
                pltpu.SemaphoreType.DMA((LAYERS,)),
                pltpu.SemaphoreType.DMA((LAYERS,)),
                pltpu.SemaphoreType.DMA((LAYERS,)),
                pltpu.SemaphoreType.DMA((LAYERS,)),
            ],
            compiler_params=pltpu.CompilerParams(
                collective_id=0, has_side_effects=True, vmem_limit_bytes=60 * 1024 * 1024),
            cost_estimate=pl.CostEstimate(flops=flops, bytes_accessed=conv_w.size * 2, transcendentals=0),
        )(lat.reshape(frames, width, channels), conv_w.reshape(LAYERS, 9, 3 * channels, channels),
          conv_b.reshape(LAYERS, 1, channels), gn_gamma.reshape(LAYERS, channels // 128, 128),
          gn_beta.reshape(LAYERS, channels // 128, 128))
        return out.reshape(lat.shape)

    video_spec = P(("dp", "cp"), "hp", None, None)
    return jax.shard_map(local_decode, mesh=mesh, in_specs=(video_spec, P(), P(), P(), P()), out_specs=video_spec, check_vma=False)
```

time: 564 us -> 117 us (0.21)
  the two profiles are of different devices: /device:TPU:34 before, /device:TPU:2 now
where the time goes in v1:
time: 117 us
  Pallas kernels  111 us (95%)
  local copies, waits for them, and re-layouts  5.83 us (5%)
    pallas_call x1, Pallas kernels, local_decode(): pl.pallas_call(functools.partial(decode_kernel, n_hp, n_cp, total_count),...  111 us

profile of v1, /device:TPU:2, one launch (start us, length us, event | category | flops | bytes accessed | tf_op | source)
XLA Modules:
  0.0 116.7 jit_solution(15696276940687645526)
XLA Ops:
  0.0 1.3 %reshape.20.b_ref = f32[4,1,512]{2,1,0:T(1,128)} reshape(f32[4,512]{1,0:T(4,128)} %param.7) | data formatting | bytes 16384 | tf_op jit(solution)/shard_map/reshape | solution.py:328
  1.3 1.3 %reshape.21.g_ref = f32[4,4,128]{2,1,0:T(4,128)} reshape(f32[4,512]{1,0:T(4,128)} %param.8) | data formatting | bytes 16384 | tf_op jit(solution)/shard_map/reshape | solution.py:328
  2.6 1.3 %reshape.22.be_ref = f32[4,4,128]{2,1,0:T(4,128)} reshape(f32[4,512]{1,0:T(4,128)} %param.9) | data formatting | bytes 16384 | tf_op jit(solution)/shard_map/reshape | solution.py:329
  3.9 110.9 %shard_map.55 = bf16[12,48,512]{2,1,0:T(8,128)(2,1)} custom-call(bf16[12,48,512]{2,1,0:T(8,128)(2,1)} %bitcast.7, bf16[4,9,1536,512]{3,2,1,0:T(8,128)(2,1)} %bitcast.6, f32[4,1,512]{2,1,0:T(1,128)} %reshape.20.b_ref, f32[4,4,128]{2,1,0:T(4,128)} %reshape.21.g_ref, f32[4,4,128]{2,1,0:T(4,128)} %reshape.22.be_ref), custom_call_target="tpu_custom_call" | custom-call | flops 32614907904 | bytes 56623104 | tf_op jit(solution)/shard_map/pallas_call | solution.py:297
  114.8 1.9 %copy.8 = bf16[12,1,48,512]{3,2,1,0:T(8,128)(2,1)} copy(bf16[12,1,48,512]{3,2,1,0:T(8,128)(2,1)} %bitcast.5) | data formatting | bytes 1179648

commit v2 on v1

v2 whole, which is shorter than its diff:
```python
import functools

import jax
import jax.numpy as jnp
from jax import lax
from jax.experimental import pallas as pl
from jax.experimental.pallas import tpu as pltpu
from jax.sharding import PartitionSpec as P

GROUPS = 32
EPS = 1e-6
LAYERS = 4
MESH = pl.DeviceIdType.MESH
CHUNK = 3


def lane_sums(y, lane):
    for d in (8, 4, 2, 1):
        y = y + jnp.where((lane & d) != 0, pltpu.roll(y, d, 1), pltpu.roll(y, 128 - d, 1))
    return y


def decode_kernel(n_hp, n_cp, total_count, lat_ref, w_ref, b_ref, g_ref, be_ref, o_ref,
                  wbuf, raw, act, acc, xres, params, ssum, st8, coef, msg, peers,
                  w_sem, lat_sem, send_sem, recv_sem, msg_send, msg_recv):
    frames, width, channels = xres.shape
    n_chunks = frames // CHUNK
    hp = lax.axis_index("hp")
    cp = lax.axis_index("cp")
    has_up = hp > 0
    has_down = hp < n_hp - 1
    has_next = cp < n_cp - 1
    has_prev = cp > 0

    for i, ref in enumerate((b_ref, g_ref, be_ref)):
        for layer in range(LAYERS):
            params[i, layer] = ref[layer : layer + 1, :]

    slab_order = [(k, 1) for k in range(3)] + [(k, di) for di in (0, 2) for k in range(3)]

    def weight_copy(layer, slot, k, di):
        slab = k * 3 + di
        return pltpu.make_async_copy(w_ref.at[layer, slab], wbuf.at[slot, slab], w_sem.at[slot, slab])

    def start_weights(layer, slot):
        for k, di in slab_order:
            weight_copy(layer, slot, k, di).start()

    lat_copies = [pltpu.make_async_copy(lat_ref, raw.at[0, 1, pl.ds(2, frames)], lat_sem.at[0]),
                  pltpu.make_async_copy(lat_ref, xres, lat_sem.at[1])]
    for copy in lat_copies:
        copy.start()
    start_weights(0, 0)

    def others(visit):
        @pl.loop(0, n_hp)
        def _(i):
            for j in range(n_cp):
                target = {"hp": lax.rem(hp + n_hp // 2 + i, n_hp), "cp": lax.rem(cp + n_cp // 2 + j, n_cp)}
                if j == n_cp // 2:
                    pl.when(i != n_hp // 2)(functools.partial(visit, target))
                else:
                    visit(target)

    barrier = pltpu.get_barrier_semaphore()
    with jax.named_scope("entry_signals"):
        others(lambda target: pl.semaphore_signal(barrier, inc=1, device_id=target, device_id_type=MESH))

    def row_copy(slot, c, to_down):
        span = pl.ds(2 + c * CHUNK, CHUNK)
        row = 0 if to_down else 2
        return pltpu.make_async_remote_copy(
            src_ref=raw.at[slot, 1, span], dst_ref=raw.at[slot, row, span],
            send_sem=send_sem.at[row, c], recv_sem=recv_sem.at[slot, row, c],
            device_id={"hp": hp + (1 if to_down else -1)}, device_id_type=MESH)

    def time_copy(slot, dh):
        row = dh if dh is None else (0 if dh == 1 else 2)
        row = 1 if dh == 0 else row
        return pltpu.make_async_remote_copy(
            src_ref=raw.at[slot, 1, pl.ds(frames, 2)], dst_ref=raw.at[slot, row, pl.ds(0, 2)],
            send_sem=send_sem.at[row, n_chunks], recv_sem=recv_sem.at[slot, row, n_chunks],
            device_id={"hp": hp + dh, "cp": cp + 1}, device_id_type=MESH)

    def start_rows(slot, c):
        @pl.when(has_up)
        def _():
            row_copy(slot, c, False).start()

        @pl.when(has_down)
        def _():
            row_copy(slot, c, True).start()

    def start_times(slot):
        @pl.when(has_next)
        def _():
            time_copy(slot, 0).start()

        @pl.when(jnp.logical_and(has_next, has_up))
        def _():
            time_copy(slot, -1).start()

        @pl.when(jnp.logical_and(has_next, has_down))
        def _():
            time_copy(slot, 1).start()

    def wait_sends(slot):
        for c in range(n_chunks):
            @pl.when(has_up)
            def _():
                row_copy(slot, c, False).wait_send()

            @pl.when(has_down)
            def _():
                row_copy(slot, c, True).wait_send()

        @pl.when(has_next)
        def _():
            time_copy(slot, 0).wait_send()

        @pl.when(jnp.logical_and(has_next, has_up))
        def _():
            time_copy(slot, -1).wait_send()

        @pl.when(jnp.logical_and(has_next, has_down))
        def _():
            time_copy(slot, 1).wait_send()

    for row, ok in ((0, has_up), (2, has_down)):
        @pl.when(jnp.logical_not(ok))
        def _():
            @pl.loop(0, frames + 2)
            def _(f):
                for slot in range(2):
                    raw[slot, row, f] = jnp.zeros((width, channels), jnp.bfloat16)

    @pl.when(jnp.logical_not(has_prev))
    def _():
        for slot in range(2):
            for row in range(3):
                for f in range(2):
                    raw[slot, row, f] = jnp.zeros((width, channels), jnp.bfloat16)

    with jax.named_scope("lat_wait"):
        for copy in lat_copies:
            copy.wait()

    def fold(v):
        return jnp.sum(v.reshape(-1, 8, v.shape[-1]), axis=0)

    ssum[...] = jnp.zeros_like(ssum)

    @pl.loop(0, frames)
    def _(f):
        v = xres[f].astype(jnp.float32)
        ssum[0] += fold(v)
        ssum[1] += fold(v * v)

    lane = lax.broadcasted_iota(jnp.int32, (8, 128), 1)
    sub = lax.broadcasted_iota(jnp.int32, (8, 128), 0)
    pick = (lane & 15) == sub

    me = hp * n_cp + cp

    def send_sums(layer):
        for s in range(2):
            for i in range(4):
                st8[s * 4 + i : s * 4 + i + 1, :] = jnp.sum(ssum[s, :, i * 128 : (i + 1) * 128], axis=0, keepdims=True)
        mine = jnp.where(pick, lane_sums(st8[...], lane), 0.0)
        msg[layer] = jnp.sum(mine, axis=0, keepdims=True)
        peers[layer, me] = msg[layer]
        others(lambda target: pltpu.make_async_remote_copy(
            src_ref=msg.at[layer], dst_ref=peers.at[layer, me], send_sem=msg_send.at[layer], recv_sem=msg_recv.at[layer],
            device_id=target, device_id_type=MESH).start())

    def statistics(layer):
        rest = peers.at[layer, pl.ds(0, n_hp * n_cp - 1)]
        pltpu.make_async_copy(rest, rest, msg_recv.at[layer]).wait()
        pltpu.make_async_copy(rest, rest, msg_send.at[layer]).wait()
        total = jnp.sum(peers[layer], axis=0)
        st8[...] = lane_sums(jnp.where(pick, jnp.broadcast_to(total, (8, 128)), 0.0), lane)
        mean = st8[0:4, :] / total_count
        var = st8[4:8, :] / total_count - mean * mean
        inv = lax.rsqrt(var + EPS)
        st8[0:4, :] = inv
        st8[4:8, :] = mean * inv
        for i in range(4):
            lanes = slice(i * 128, (i + 1) * 128)
            gamma = 0.5 * params[1, layer, :, lanes]
            scale = gamma * st8[i : i + 1, :]
            shift = 0.5 * params[2, layer, :, lanes] - st8[4 + i : 5 + i, :] * gamma
            for row, ok in ((0, has_up), (1, None), (2, has_down)):
                coef[row, 0:1, lanes] = scale if ok is None else jnp.where(ok, scale, 0.0)
                coef[row, 1:2, lanes] = shift if ok is None else jnp.where(ok, shift, 0.0)

    first_frame = jnp.where(has_prev, 0, 2)
    col = lax.broadcasted_iota(jnp.int32, (width, channels), 0)

    def activate(slot, row, f):
        v = raw[slot, row, jnp.maximum(f, first_frame)].astype(jnp.float32)
        u = v * coef[row, 0:1, :] + coef[row, 1:2, :]
        y = u * jnp.tanh(u) + u
        left = jnp.where(col == 0, 0.0, pltpu.roll(y, 1, 0))
        right = jnp.where(col == width - 1, 0.0, pltpu.roll(y, width - 1, 0))
        for dj, v in enumerate((left, y, right)):
            act[row, f, :, dj * channels : (dj + 1) * channels] = v.astype(jnp.bfloat16)

    def taps(slot, di, start, count):
        total = None
        for d in di:
            for k in range(3):
                lhs = act[d, pl.ds(start + k, count)].reshape(count * width, 3 * channels)
                part = jnp.dot(lhs, wbuf[slot, k * 3 + d], preferred_element_type=jnp.float32)
                total = part if total is None else total + part
        return total

    def halo_wait(slot, c):
        for row, ok in ((0, has_up), (2, has_down)):
            if c == 0:
                @pl.when(jnp.logical_and(ok, has_prev))
                def _():
                    time_copy(slot, 1 if row == 0 else -1).wait_recv()

            @pl.when(ok)
            def _():
                row_copy(slot, c, row == 0).wait_recv()

    def halo_act(slot, c):
        for f in range(2 + c * CHUNK if c else 0, 2 + (c + 1) * CHUNK):
            for row in (0, 2):
                activate(slot, row, f)

    def finish(layer, other, c):
        second = lax.rem(layer, 2) == 1
        for f in range(c * CHUNK, (c + 1) * CHUNK):
            h = (acc[f] + params[0, layer]).astype(jnp.bfloat16).astype(jnp.float32)
            x = xres[f].astype(jnp.float32)
            out = (h + jnp.where(second, x, 0.0)).astype(jnp.bfloat16)
            raw[other, 1, 2 + f] = out
            out = out.astype(jnp.float32)
            xres[f] = jnp.where(second, out, x).astype(jnp.bfloat16)
            ssum[0] += fold(out)
            ssum[1] += fold(out * out)

    with jax.named_scope("entry_wait"):
        pl.semaphore_wait(barrier, n_hp * n_cp - 1)
    with jax.named_scope("send_sums"):
        send_sums(0)
    start_times(0)
    for c in range(n_chunks):
        start_rows(0, c)

    def layer_body(layer, _):
        slot = lax.rem(layer, 2)
        other = 1 - slot
        more = layer < LAYERS - 1

        @pl.when(more)
        def _():
            start_weights(layer + 1, other)

        with jax.named_scope("statistics"):
            statistics(layer)

        with jax.named_scope("act_own"):
            @pl.when(has_prev)
            def _():
                time_copy(slot, 0).wait_recv()

            @pl.loop(0, frames + 2)
            def _(f):
                activate(slot, 1, f)

        with jax.named_scope("w_wait"):
            for k, di in slab_order:
                weight_copy(layer, slot, k, di).wait()

        half = frames // 2
        with jax.named_scope("own0"):
            acc[0:half] = taps(slot, (1,), 0, half).reshape(half, width, channels)
        with jax.named_scope("halo_wait0"):
            halo_wait(slot, 0)
        with jax.named_scope("own1"):
            halo_act(slot, 0)
            acc[half:frames] = taps(slot, (1,), half, half).reshape(half, width, channels)
        with jax.named_scope("send_wait"):
            wait_sends(slot)
        ssum[...] = jnp.zeros_like(ssum)
        for c in range(n_chunks):
            if c < n_chunks - 1:
                with jax.named_scope(f"halo_wait{c + 1}"):
                    halo_wait(slot, c + 1)
            span = slice(c * CHUNK, (c + 1) * CHUNK)
            with jax.named_scope(f"chunk{c}"):
                if c > 0:
                    finish(layer, other, c - 1)
                if c < n_chunks - 1:
                    halo_act(slot, c + 1)
                acc[span] += taps(slot, (0, 2), c * CHUNK, CHUNK).reshape(CHUNK, width, channels)
            if c == 1:
                @pl.when(more)
                def _():
                    start_rows(other, 0)

        with jax.named_scope("finish"):
            finish(layer, other, n_chunks - 1)

        @pl.when(more)
        def _():
            with jax.named_scope("send_sums"):
                send_sums(layer + 1)
            with jax.named_scope("send_rest"):
                start_times(other)
                for c in range(1, n_chunks):
                    start_rows(other, c)

        return 0

    lax.fori_loop(0, LAYERS, layer_body, 0)

    @pl.loop(0, frames)
    def _(f):
        o_ref[f] = xres[f]


def solution(mesh):
    n_hp, n_cp = mesh.shape["hp"], mesh.shape["cp"]

    def local_decode(lat, conv_w, conv_b, gn_gamma, gn_beta):
        frames, rows, width, channels = lat.shape
        n_chunks = frames // CHUNK
        total_count = float(frames * n_cp * rows * n_hp * width * (channels // GROUPS))
        any_spec = pl.BlockSpec(memory_space=pl.ANY)
        vmem_spec = pl.BlockSpec(memory_space=pltpu.VMEM)
        bf16, f32 = jnp.bfloat16, jnp.float32
        flops = LAYERS * 2 * frames * width * 27 * channels * channels
        out = pl.pallas_call(
            functools.partial(decode_kernel, n_hp, n_cp, total_count),
            out_shape=jax.ShapeDtypeStruct((frames, width, channels), bf16),
            in_specs=[any_spec, any_spec, vmem_spec, vmem_spec, vmem_spec],
            out_specs=vmem_spec,
            scratch_shapes=[
                pltpu.VMEM((2, 9, 3 * channels, channels), bf16),
                pltpu.VMEM((2, 3, frames + 2, width, channels), bf16),
                pltpu.VMEM((3, frames + 2, width, 3 * channels), bf16),
                pltpu.VMEM((frames, width, channels), f32),
                pltpu.VMEM((frames, width, channels), bf16),
                pltpu.VMEM((3, LAYERS, 1, channels), f32),
                pltpu.VMEM((2, 8, channels), f32),
                pltpu.VMEM((8, 128), f32),
                pltpu.VMEM((3, 8, channels), f32),
                pltpu.VMEM((LAYERS, 1, 128), f32),
                pltpu.VMEM((LAYERS, n_hp * n_cp, 1, 128), f32),
                pltpu.SemaphoreType.DMA((2, 9)),
                pltpu.SemaphoreType.DMA((2,)),
                pltpu.SemaphoreType.DMA((3, n_chunks + 1)),
                pltpu.SemaphoreType.DMA((2, 3, n_chunks + 1)),
                pltpu.SemaphoreType.DMA((LAYERS,)),
                pltpu.SemaphoreType.DMA((LAYERS,)),
            ],
            compiler_params=pltpu.CompilerParams(
                collective_id=0, has_side_effects=True, vmem_limit_bytes=60 * 1024 * 1024),
            cost_estimate=pl.CostEstimate(flops=flops, bytes_accessed=conv_w.size * 2, transcendentals=0),
        )(lat.reshape(frames, width, channels), conv_w.reshape(LAYERS, 9, 3 * channels, channels),
          conv_b, gn_gamma, gn_beta)
        return out.reshape(lat.shape)

    video_spec = P(("dp", "cp"), "hp", None, None)
    return jax.shard_map(local_decode, mesh=mesh, in_specs=(video_spec, P(), P(), P(), P()), out_specs=video_spec, check_vma=False)
```

time: 117 us -> 98.8 us (0.84)
  the two profiles are of different devices: /device:TPU:2 before, /device:TPU:1 now
where the time goes in v2:
time: 98.8 us; the launch traced here: 98.7 us
  Pallas kernels  96.7 us (98%)
  local copies, waits for them, and re-layouts  1.92 us (2%)
    pallas_call x1, Pallas kernels, local_decode(): pl.pallas_call(functools.partial(decode_kernel, n_hp, n_cp, total_count),...  96.7 us

profile of v2, /device:TPU:1, one launch (start us, length us, event | category | flops | bytes accessed | tf_op | source)
XLA Modules:
  0.0 98.7 jit_solution(9612409171815091497)
XLA Ops:
  0.0 96.7 %shard_map.55 = bf16[12,48,512]{2,1,0:T(8,128)(2,1)} custom-call(bf16[12,48,512]{2,1,0:T(8,128)(2,1)} %bitcast.7, bf16[4,9,1536,512]{3,2,1,0:T(8,128)(2,1)} %bitcast.6, f32[4,512]{1,0:T(4,128)} %b_ref.1, f32[4,512]{1,0:T(4,128)} %g_ref.1, f32[4,512]{1,0:T(4,128)} %be_ref.1), custom_call_target="tpu_custom_call" | custom-call | flops 32614907904 | bytes 56623104 | tf_op jit(solution)/shard_map/pallas_call | solution.py:337
  96.7 1.9 %copy.8 = bf16[12,1,48,512]{3,2,1,0:T(8,128)(2,1)} copy(bf16[12,1,48,512]{3,2,1,0:T(8,128)(2,1)} %bitcast.5) | data formatting | bytes 1179648
